TPU v7x, 32 devices: a whole 2x2x4 slice. The times are simulated.
32 devices in a mesh: gx: 4 (over y, core), gy: 8 (over z, x).
Axes of the slice: x: 2, y: 2, z: 4, core: 2. Of those that a mesh axis runs over, the one named last changes fastest.
Arguments:
- previous: float32 [2, 7, 512, 1024], P(None, None, 'gx', 'gy'), may hold values from -6 to 6
- dissipated: float32 [2, 4, 512, 1024], P(None, None, 'gx', 'gy'), may hold values from 0.05 to 3
- material: int32 [4, 512, 1024], P(None, 'gx', 'gy'), may hold values from 0 to 3
- coolant: int32 [3, 512, 1024], P(None, 'gx', 'gy'), may hold values from 0 to 3
Outputs:
- temperature: float32 [2, 7, 512, 1024], P(None, None, 'gx', 'gy')
All inputs are finite; a program needn't handle non-finite values.
Results may differ from a plain program's by a relative error of at most 0.00011.
Values sent between devices are 32-bit elements; how exact they have to be, the bound alone decides.
A program may use at most 64 MiB of HBM per device.

v0:
```python
import jax
import jax.numpy as jnp
from jax import lax
from jax.sharding import PartitionSpec as P

ITERS = 3
TIER_K = (1.0, 0.3, 0.12, 2.5)
CHANNEL_K = (1.0, 0.3, 0.25, 0.2)
CHANNEL_SINK = (0.0, 0.15, 0.45, 1.2)
TIER_HEAT = 0.05
CHANNEL_HEAT = 0.2
VERTICAL = 4.0


def extended_2(x, sides, width):
    for axis, dim in sides:
        devices, length = (lax.axis_size(axis), x.shape[dim])
        up = [(i, (i + 1) % devices) for i in range(devices - 1)]
        down = [(j, i) for i, j in up]
        last = lax.slice_in_dim(x, length - width, length, axis=dim)
        leading = lax.slice_in_dim(x, 0, width, axis=dim)
        before = lax.ppermute(last, axis, up)
        after = lax.ppermute(leading, axis, down)
        x = jnp.concatenate([before, x, after], axis=dim)
    return x


def lookup(codes, table):
    total = jnp.zeros(codes.shape, jnp.float32)
    for index, value in enumerate(table):
        total = total + jnp.where(codes == index, jnp.float32(value), jnp.float32(0.0))
    return total


def mix(tiers, channels):
    rows = []
    for layer in range(2 * tiers.shape[0] - 1):
        rows.append(tiers[layer // 2] if layer % 2 == 0 else channels[layer // 2])
    return jnp.stack(rows)


def spread_power(heat):
    tiers = heat.shape[1]
    empty = jnp.zeros_like(heat[:, 0])
    rows = []
    for layer in range(2 * tiers - 1):
        rows.append(heat[:, layer // 2] if layer % 2 == 0 else empty)
    return jnp.stack(rows, 1)


def capacity_column(layers):
    return jnp.array(
        [TIER_HEAT if layer % 2 == 0 else CHANNEL_HEAT for layer in range(layers)], jnp.float32
    )


def couplings(padded_k):
    centre = padded_k[:, 1:-1, 1:-1]
    g_north = jnp.sqrt(centre * padded_k[:, :-2, 1:-1])
    g_south = jnp.sqrt(centre * padded_k[:, 2:, 1:-1])
    g_west = jnp.sqrt(centre * padded_k[:, 1:-1, :-2])
    g_east = jnp.sqrt(centre * padded_k[:, 1:-1, 2:])
    g_vertical = VERTICAL * jnp.sqrt(centre[:-1] * centre[1:])
    return (g_north, g_south, g_west, g_east, g_vertical)


def operate(padded_v, padded_k, sink, capacity):
    g_north, g_south, g_west, g_east, g_vertical = couplings(padded_k)
    centre = padded_v[:, :, 1:-1, 1:-1]
    lateral = g_north * (centre - padded_v[:, :, :-2, 1:-1]) + g_south * (
        centre - padded_v[:, :, 2:, 1:-1]
    )
    lateral = (
        lateral
        + g_west * (centre - padded_v[:, :, 1:-1, :-2])
        + g_east * (centre - padded_v[:, :, 1:-1, 2:])
    )
    flux = g_vertical * (centre[:, :-1] - centre[:, 1:])
    zero_row = jnp.zeros_like(centre[:, :1])
    vertical = jnp.concatenate([flux, zero_row], 1) - jnp.concatenate([zero_row, flux], 1)
    return (capacity + sink) * centre + lateral + vertical


def diagonal_terms(padded_k, sink, capacity):
    g_north, g_south, g_west, g_east, g_vertical = couplings(padded_k)
    zero_row = jnp.zeros_like(g_vertical[:1])
    vertical = jnp.concatenate([g_vertical, zero_row], 0) + jnp.concatenate(
        [zero_row, g_vertical], 0
    )
    return capacity + sink + g_north + g_south + g_west + g_east + vertical


def core_sum(first, second):
    return jnp.sum(first * second, axis=(1, 2, 3))


def both_sums(residual, scaled, image):
    return lax.psum((core_sum(residual, scaled), core_sum(scaled, image)), ("gx", "gy"))


def per_device(previous, dissipated, material, coolant):
    tiers = material.shape[0]
    layers = 2 * tiers - 1
    capacity = capacity_column(layers)[:, None, None]
    tier_k = lookup(material, TIER_K)
    kappa = mix(tier_k, lookup(coolant, CHANNEL_K))
    channel_sink = lookup(coolant, CHANNEL_SINK)
    conductivity = extended_2(kappa, (("gx", 1), ("gy", 2)), 1)
    coolant_sink = mix(jnp.zeros_like(tier_k), channel_sink)
    margin_start = 0

    def apply_operator(field, margin):
        extended = extended_2(field, (("gx", 2), ("gy", 3)), 1)
        result = operate(extended, conductivity, coolant_sink, capacity)
        return (result, margin)

    diagonal = diagonal_terms(conductivity, coolant_sink, capacity)
    source = capacity * previous + spread_power(dissipated)
    image, margin = apply_operator(previous, margin_start)
    residual = source - image
    solution = previous
    scaled = residual / diagonal
    image, inner_margin = apply_operator(scaled, margin)
    energy, curvature_now = both_sums(residual, scaled, image)
    step_size = energy / curvature_now
    direction = scaled
    along = image
    margin = inner_margin
    for iteration in range(ITERS):
        solution = solution + step_size[:, None, None, None] * direction
        residual = residual - step_size[:, None, None, None] * along
        if iteration + 1 < ITERS:
            scaled = residual / diagonal
            image, inner_margin = apply_operator(scaled, margin)
            energy_next, curvature_now = both_sums(residual, scaled, image)
            growth = energy_next / energy
            step_size = energy_next / (curvature_now - growth * energy_next / step_size)
            factor = growth[:, None, None, None]
            direction = scaled + factor * direction
            along = image + factor * along
            margin = inner_margin
            energy = energy_next
    return solution


def solution(mesh):
    return jax.shard_map(
        per_device,
        mesh=mesh,
        in_specs=(
            P(None, None, "gx", "gy"),
            P(None, None, "gx", "gy"),
            P(None, "gx", "gy"),
            P(None, "gx", "gy"),
        ),
        out_specs=P(None, None, "gx", "gy"),
        check_vma=False,
    )
```

profile of v0, /device:TPU:0, one launch (start us, length us, event | category | flops | bytes accessed | tf_op | source)
XLA Modules:
  0.0 283.8 jit_solution(1892046935967206937)
XLA Ops:
  3.3 3.7 %collective-permute-start.1 = (f32[2,7,1,128]{3,1,2,0:T(8,128)}, f32[2,7,1,128]{3,1,2,0:T(8,128)}, u32[]{:S(2)}, u32[]{:S(2)}) collective-permute-start(f32[2,7,1,128]{3,1,2,0:T(8,128)} %copy.160), channel_id=1, source_target_pairs={{0,8},{8,16},{16,24},{1,9},{9,17},{17,25},{2,10},{10,18},{18,26},{... | collective-permute-start | bytes 21512 | tf_op jit(solution)/shard_map/ppermute | solution.py:22
  10.3 4.6 %collective-permute-start = (f32[7,1,128]{2,1,0:T(1,128)}, f32[7,1,128]{2,1,0:T(1,128)S(1)}, u32[]{:S(2)}, u32[]{:S(2)}) collective-permute-start(f32[7,1,128]{2,1,0:T(1,128)} %get-tuple-element.55), channel_id=1, source_target_pairs={{0,8},{8,16},{16,24},{1,9},{9,17},{17,25},{2,10},{10,18},{18,26},{... | collective-permute-start | bytes 10760 | tf_op jit(solution)/shard_map/ppermute | solution.py:22
  27.0 2.4 stack.15
  32.4 5.4 %collective-permute-start.4 = (f32[7,130,1]{2,1,0:T(8,128)}, f32[7,130,1]{2,1,0:T(8,128)}, u32[]{:S(2)}, u32[]{:S(2)}) collective-permute-start(f32[7,130,1]{2,1,0:T(8,128)} %get-tuple-element.52), channel_id=1, source_target_pairs={{0,1},{1,2},{2,3},{3,4},{4,5},{5,6},{6,7},{8,9},{9,10},{10,11},{11... | collective-permute-start | bytes 10928 | tf_op jit(solution)/shard_map/ppermute | solution.py:22
  40.3 3.6 %collective-permute-start.5 = (f32[2,7,130,1]{2,1,3,0:T(8,128)}, f32[2,7,130,1]{2,1,3,0:T(8,128)S(1)}, u32[]{:S(2)}, u32[]{:S(2)}) collective-permute-start(f32[2,7,130,1]{2,1,3,0:T(8,128)} %get-tuple-element.37), channel_id=1, source_target_pairs={{0,1},{1,2},{2,3},{3,4},{4,5},{5,6},{6,7},{8,9},{9,10},{10,11},{11... | collective-permute-start | bytes 21848 | tf_op jit(solution)/shard_map/ppermute | solution.py:22
  45.3 1.3 collective-permute-done.6
  46.6 11.4 %collective-permute-done.4 = f32[7,130,1]{2,1,0:T(8,128)} collective-permute-done((f32[7,130,1]{2,1,0:T(8,128)}, f32[7,130,1]{2,1,0:T(8,128)}, u32[]{:S(2)}, u32[]{:S(2)}) %collective-permute-start.4) | collective-permute-done | bytes 3672 | tf_op jit(solution)/shard_map/ppermute | solution.py:22
  58.0 3.0 %add_add_fusion = (f32[7,128,128]{2,1,0:T(8,128)}, f32[7,128,128]{2,1,0:T(8,128)}, f32[7,128,128]{2,1,0:T(8,128)S(1)}, f32[7,128,128]{2,1,0:T(8,128)S(1)}, f32[7...) fusion(f32[6,128,128]{2,1,0:T(8,128)S(1)} %sqrt_multiply_fusion, f32[7,128,128]{2,1,0:T(8,128)S(1)} %copy-done.33, ...), kind=kLoop, calls=%fused_computation.123 | loop fusion | flops 2179072 | bytes 4077708 | tf_op jit(solution)/shard_map/add | solution.py:90
  61.0 2.1 copy.139
  68.2 5.3 %broadcast_divide_fusion.2 = (f32[2,7,128,128]{2,1,3,0:T(8,128)S(1)}, f32[2,7,128,128]{2,1,3,0:T(8,128)S(1)}) fusion(f32[7,128,128]{1,0,2:T(8,128)} %copy.139, f32[2,6,128,128]{2,1,3,0:T(8,128)} %fusion.44, f32[2,7,128,128]{2,1,3,0:T(8,128)S(1)} %copy.146, f32[2,7,130,1]{2,1,3,0:T(8,128)} %collective-permute-done.7, f32[2,7,1,128]{2,1,3,0:T(8,128)} %copy-done.26, ...), kind=kLoop, calls=%fused_computation.105 | loop fusion | flops 6193152 | bytes 7237884 | tf_op jit(solution)/shard_map/div | solution.py:122
  73.6 1.3 fusion.77
  75.0 1.6 copy.140
  76.5 2.1 collective-permute-start.8
  79.0 1.3 collective-permute-start.9
  80.3 1.4 copy.141
  82.1 1.4 copy.143
  84.4 4.3 %collective-permute-start.10 = (f32[2,7,130,1]{2,1,3,0:T(8,128)S(1)}, f32[2,7,130,1]{2,1,3,0:T(8,128)S(1)}, u32[]{:S(2)}, u32[]{:S(2)}) collective-permute-start(f32[2,7,130,1]{2,1,3,0:T(8,128)S(1)} %get-tuple-element.35), channel_id=1, source_target_pairs={{0,1},{1,2},{2,3},{3,4},{4,5},{5,6},{6,7},{8,9},{9,10},{10,11},{11... | collective-permute-start | bytes 21848 | tf_op jit(solution)/shard_map/ppermute | solution.py:22
  88.7 1.6 collective-permute-start.11
  90.5 4.2 %collective-permute-done.11 = f32[2,7,130,1]{2,1,3,0:T(8,128)S(1)} collective-permute-done((f32[2,7,130,1]{2,1,3,0:T(8,128)S(1)}, f32[2,7,130,1]{2,1,3,0:T(8,128)S(1)}, u32[]{:S(2)}, u32[]{:S(2)}) %collective-permute-start.11) | collective-permute-done | bytes 7312 | tf_op jit(solution)/shard_map/ppermute | solution.py:23
  94.7 3.0 %multiply_reduce_fusion.3 = (f32[2]{0:T(128)S(1)}, f32[2]{0:T(128)S(1)}, f32[2,7,128,128]{2,1,3,0:T(8,128)}) fusion(f32[2,7,128,128]{2,1,3,0:T(8,128)S(1)} %get-tuple-element.24, f32[2,7,128,128]{2,1,3,0:T(8,128)S(1)} %get-tuple-element.25, f32[2,6,128,128]{2,1,3,0:T(8,128)S(1)} %fusion.30, f32[2,7,130,1]{2,1,3,0:T(8,128)S(1)} %collective-permute-done.11, ...), kind=kLoop, calls=%fused_computation.101 | loop fusion | flops 6193148 | bytes 5861616 | tf_op jit(solution)/shard_map/reduce_sum | solution.py:94
  97.7 40.7 %all-reduce.12 = (f32[2]{0:T(128)S(1)}, f32[2]{0:T(128)S(1)}) all-reduce(f32[2]{0:T(128)S(1)} %get-tuple-element.8, f32[2]{0:T(128)S(1)} %get-tuple-element.7), channel_id=1, replica_groups=mesh['gx'=4,'gy'=8] {'gx','gy'}, use_global_device_ids=true, to_apply=%region_1.2 | all-reduce | flops 4 | bytes 32 | tf_op jit(solution)/shard_map/psum | solution.py:98
  138.5 1.6 broadcast_divide_fusion.1
  140.1 1.7 fusion.76
  141.7 1.6 copy.147
  144.6 1.6 copy.149
  146.1 1.5 collective-permute-start.13
  147.6 1.4 copy.148
  149.0 2.7 collective-permute-done.13
  151.7 1.4 copy.150
  154.1 2.5 collective-permute-start.14
  156.6 1.6 collective-permute-start.15
  158.3 4.2 %collective-permute-done.15 = f32[2,7,130,1]{2,1,3,0:T(8,128)S(1)} collective-permute-done((f32[2,7,130,1]{2,1,3,0:T(8,128)S(1)}, f32[2,7,130,1]{2,1,3,0:T(8,128)S(1)}, u32[]{:S(2)}, u32[]{:S(2)}) %collective-permute-start.15) | collective-permute-done | bytes 7312 | tf_op jit(solution)/shard_map/ppermute | solution.py:23
  162.6 3.2 %multiply_reduce_fusion.1 = (f32[2]{0:T(128)S(1)}, f32[2]{0:T(128)S(1)}, f32[2,7,128,128]{2,1,3,0:T(8,128)}) fusion(f32[2,7,128,128]{2,1,3,0:T(8,128)S(1)} %broadcast_divide_fusion.1, f32[2,7,128,128]{2,1,3,0:T(8,128)S(1)} %get-tuple-element.25, f32[2,7,128,128]{2,1,3,0:T(8,128)S(1)} %copy-done.3, f32[2]{0:T(128)S(1)} %div.43, ...), kind=kLoop, calls=%fused_computation.98 | loop fusion | flops 6651900 | bytes 6779128 | tf_op jit(solution)/shard_map/reduce_sum | solution.py:94
  165.7 42.0 %all-reduce.11 = (f32[2]{0:T(128)S(1)}, f32[2]{0:T(128)S(1)}) all-reduce(f32[2]{0:T(128)S(1)} %get-tuple-element.6, f32[2]{0:T(128)S(1)} %get-tuple-element.5), channel_id=1, replica_groups=mesh['gx'=4,'gy'=8] {'gx','gy'}, use_global_device_ids=true, to_apply=%region_5.6 | all-reduce | flops 4 | bytes 32 | tf_op jit(solution)/shard_map/psum | solution.py:98
  207.7 3.4 %broadcast_divide_fusion = (f32[2,7,128,128]{2,1,3,0:T(8,128)S(1)}, f32[2,7,128,128]{2,1,3,0:T(8,128)}) fusion(f32[7,128,128]{1,0,2:T(8,128)} %copy.139, f32[2,7,128,128]{2,1,3,0:T(8,128)} %get-tuple-element.22, f32[2,7,128,128]{2,1,3,0:T(8,128)} %get-tuple-element.23, f32[2]{0:T(128)S(1)} %get-tuple-element.21, f32[2]{0:T(128)S(1)} %get-tuple-element.19, ...), kind=kLoop, calls=%fused_computation.103 | loop fusion | flops 1605632 | bytes 5046296 | tf_op jit(solution)/shard_map/div | solution.py:133
  211.1 1.7 fusion.75
  212.7 1.6 copy.153
  214.3 1.6 copy.155
  215.9 1.3 collective-permute-start.17
  217.2 3.0 %collective-permute-start.16 = (f32[2,7,1,128]{3,1,2,0:T(8,128)S(1)}, f32[2,7,1,128]{3,1,2,0:T(8,128)S(1)}, u32[]{:S(2)}, u32[]{:S(2)}) collective-permute-start(f32[2,7,1,128]{3,1,2,0:T(8,128)S(1)} %copy.153), channel_id=1, source_target_pairs={{0,8},{8,16},{16,24},{1,9},{9,17},{17,25},{2,10},{10,18},{18,26},{... | collective-permute-start | bytes 21512 | tf_op jit(solution)/shard_map/ppermute | solution.py:22
  220.2 2.2 fusion
  222.4 1.4 copy.154
  223.7 1.4 copy.156
  226.1 4.2 %collective-permute-start.18 = (f32[2,7,130,1]{2,1,3,0:T(8,128)S(1)}, f32[2,7,130,1]{2,1,3,0:T(8,128)S(1)}, u32[]{:S(2)}, u32[]{:S(2)}) collective-permute-start(f32[2,7,130,1]{2,1,3,0:T(8,128)S(1)} %get-tuple-element.31), channel_id=1, source_target_pairs={{0,1},{1,2},{2,3},{3,4},{4,5},{5,6},{6,7},{8,9},{9,10},{10,11},{11... | collective-permute-start | bytes 21848 | tf_op jit(solution)/shard_map/ppermute | solution.py:22
  231.9 4.0 %collective-permute-done.19 = f32[2,7,130,1]{2,1,3,0:T(8,128)S(1)} collective-permute-done((f32[2,7,130,1]{2,1,3,0:T(8,128)S(1)}, f32[2,7,130,1]{2,1,3,0:T(8,128)S(1)}, u32[]{:S(2)}, u32[]{:S(2)}) %collective-permute-start.19) | collective-permute-done | bytes 7312 | tf_op jit(solution)/shard_map/ppermute | solution.py:23
  235.9 4.1 %fusion.7 = f32[2]{0:T(128)S(1)} fusion(f32[2,7,128,128]{2,1,3,0:T(8,128)S(1)} %get-tuple-element.17, f32[2,7,130,1]{2,1,3,0:T(8,128)S(1)} %collective-permute-done.19, f32[2,7,1,128]{2,1,3,0:T(8,128)} %copy.156, f32[2,7,1,128]{2,1,3,0:T(8,128)} %copy.154, f32[2,7,130,1]{2,1,3,0:T(8,128)S(1)} %collective-permute-done.18, f32[2,6,128,128]{2,1,3,0:T(8,128)} %fusion, ...), kind=kLoop, calls=%fused_computation.9 | loop fusion | flops 5734398 | bytes 4026600 | tf_op jit(solution)/shard_map/reduce_sum | solution.py:94
  240.0 40.4 %all-reduce.10 = (f32[2]{0:T(128)S(1)}, f32[2]{0:T(128)S(1)}) all-reduce(f32[2]{0:T(128)S(1)} %multiply_reduce_fusion, f32[2]{0:T(128)S(1)} %fusion.7), channel_id=1, replica_groups=mesh['gx'=4,'gy'=8] {'gx','gy'}, use_global_device_ids=true, to_apply=%region_9.10 | all-reduce | flops 4 | bytes 32 | tf_op jit(solution)/shard_map/psum | solution.py:98
  280.4 2.1 multiply_add_fusion
  (165 shorter events, 38.5 us)
Async XLA Ops:
  1.5 37.4 %collective-permute-start.3 = (f32[2,7,1,128]{3,1,2,0:T(8,128)}, f32[2,7,1,128]{3,1,2,0:T(8,128)S(1)}, u32[]{:S(2)}, u32[]{:S(2)}) collective-permute-start(f32[2,7,1,128]{3,1,2,0:T(8,128)} %copy.161), channel_id=1, source_target_pairs={{8,0},{16,8},{24,16},{9,1},{17,9},{25,17},{10,2},{18,10},{26,18},{... | collective-permute-start | bytes 21512 | tf_op jit(solution)/shard_map/ppermute | solution.py:23
  3.3 34.5 %collective-permute-start.1 = (f32[2,7,1,128]{3,1,2,0:T(8,128)}, f32[2,7,1,128]{3,1,2,0:T(8,128)}, u32[]{:S(2)}, u32[]{:S(2)}) collective-permute-start(f32[2,7,1,128]{3,1,2,0:T(8,128)} %copy.160), channel_id=1, source_target_pairs={{0,8},{8,16},{16,24},{1,9},{9,17},{17,25},{2,10},{10,18},{18,26},{... | collective-permute-start | bytes 21512 | tf_op jit(solution)/shard_map/ppermute | solution.py:22
  8.1 7.4 %copy-start.32 = (f32[2,7,128,128]{3,2,1,0:T(8,128)S(1)}, f32[2,7,128,128]{3,2,1,0:T(8,128)}, u32[]{:S(2)}) copy-start(f32[2,7,128,128]{3,2,1,0:T(8,128)} %param.5) | copy-start | bytes 2752516
  8.4 6.5 %copy-start.34 = (f32[6,128,128]{2,1,0:T(8,128)}, f32[6,128,128]{2,1,0:T(8,128)S(1)}, u32[]{:S(2)}) copy-start(f32[6,128,128]{2,1,0:T(8,128)S(1)} %get-tuple-element.58) | copy-start | bytes 1179652
  8.4 6.5 %copy-start.36 = (f32[6,128,128]{2,1,0:T(8,128)}, f32[6,128,128]{2,1,0:T(8,128)S(1)}, u32[]{:S(2)}) copy-start(f32[6,128,128]{2,1,0:T(8,128)S(1)} %get-tuple-element.57) | copy-start | bytes 1179652
  8.4 21.0 %copy-start.29 = (f32[7,128,128]{2,1,0:T(8,128)}, f32[7,128,128]{2,1,0:T(8,128)S(1)}, u32[]{:S(2)}) copy-start(f32[7,128,128]{2,1,0:T(8,128)S(1)} %get-tuple-element.56) | copy-start | bytes 1376260
  9.0 20.4 %collective-permute-start.2 = (f32[7,1,128]{2,1,0:T(1,128)}, f32[7,1,128]{2,1,0:T(1,128)S(1)}, u32[]{:S(2)}, u32[]{:S(2)}) collective-permute-start(f32[7,1,128]{2,1,0:T(1,128)} %get-tuple-element.54), channel_id=1, source_target_pairs={{8,0},{16,8},{24,16},{9,1},{17,9},{25,17},{10,2},{18,10},{26,18},{... | collective-permute-start | bytes 10760 | tf_op jit(solution)/shard_map/ppermute | solution.py:23
  10.3 19.1 %collective-permute-start = (f32[7,1,128]{2,1,0:T(1,128)}, f32[7,1,128]{2,1,0:T(1,128)S(1)}, u32[]{:S(2)}, u32[]{:S(2)}) collective-permute-start(f32[7,1,128]{2,1,0:T(1,128)} %get-tuple-element.55), channel_id=1, source_target_pairs={{0,8},{8,16},{16,24},{1,9},{9,17},{17,25},{2,10},{10,18},{18,26},{... | collective-permute-start | bytes 10760 | tf_op jit(solution)/shard_map/ppermute | solution.py:22
  15.9 52.3 %copy-start = (f32[2,7,128,128]{2,1,3,0:T(8,128)}, f32[2,7,128,128]{2,1,3,0:T(8,128)S(1)}, u32[]{:S(2)}) copy-start(f32[2,7,128,128]{2,1,3,0:T(8,128)S(1)} %copy.146) | copy-start | bytes 2752516
  31.1 15.4 %collective-permute-start.6 = (f32[7,130,1]{2,1,0:T(8,128)}, f32[7,130,1]{2,1,0:T(8,128)}, u32[]{:S(2)}, u32[]{:S(2)}) collective-permute-start(f32[7,130,1]{2,1,0:T(8,128)} %get-tuple-element.51), channel_id=1, source_target_pairs={{1,0},{2,1},{3,2},{4,3},{5,4},{6,5},{7,6},{9,8},{10,9},{11,10},{12... | collective-permute-start | bytes 10928 | tf_op jit(solution)/shard_map/ppermute | solution.py:23
  32.4 25.6 %collective-permute-start.4 = (f32[7,130,1]{2,1,0:T(8,128)}, f32[7,130,1]{2,1,0:T(8,128)}, u32[]{:S(2)}, u32[]{:S(2)}) collective-permute-start(f32[7,130,1]{2,1,0:T(8,128)} %get-tuple-element.52), channel_id=1, source_target_pairs={{0,1},{1,2},{2,3},{3,4},{4,5},{5,6},{6,7},{8,9},{9,10},{10,11},{11... | collective-permute-start | bytes 10928 | tf_op jit(solution)/shard_map/ppermute | solution.py:22
  39.3 18.7 %copy-start.30 = (f32[7,128,128]{2,1,0:T(8,128)S(1)}, f32[7,128,128]{2,1,0:T(8,128)}, u32[]{:S(2)}) copy-start(f32[7,128,128]{2,1,0:T(8,128)} %copy-done.29) | copy-start | bytes 1376260
  39.3 18.7 %copy-start.33 = (f32[7,128,128]{2,1,0:T(8,128)S(1)}, f32[7,128,128]{2,1,0:T(8,128)}, u32[]{:S(2)}) copy-start(f32[7,128,128]{2,1,0:T(8,128)} %constant_dynamic-update-slice_fusion) | copy-start | bytes 1376260
  39.3 18.7 %copy-start.42 = (f32[7,1,128]{2,1,0:T(1,128)S(1)}, f32[7,1,128]{2,1,0:T(1,128)}, u32[]{:S(2)}) copy-start(f32[7,1,128]{2,1,0:T(1,128)} %copy-done.41) | copy-start | bytes 10756
  39.4 18.7 %copy-start.43 = (f32[7]{0:T(128)S(1)}, f32[7]{0:T(128)}, u32[]{:S(2)}) copy-start(f32[7]{0:T(128)} %constant.10.clone) | copy-start | bytes 88
  40.3 17.7 %copy-start.40 = (f32[7,1,128]{2,1,0:T(1,128)S(1)}, f32[7,1,128]{2,1,0:T(1,128)}, u32[]{:S(2)}) copy-start(f32[7,1,128]{2,1,0:T(1,128)} %copy-done.39) | copy-start | bytes 10756
  40.3 27.9 %collective-permute-start.5 = (f32[2,7,130,1]{2,1,3,0:T(8,128)}, f32[2,7,130,1]{2,1,3,0:T(8,128)S(1)}, u32[]{:S(2)}, u32[]{:S(2)}) collective-permute-start(f32[2,7,130,1]{2,1,3,0:T(8,128)} %get-tuple-element.37), channel_id=1, source_target_pairs={{0,1},{1,2},{2,3},{3,4},{4,5},{5,6},{6,7},{8,9},{9,10},{10,11},{11... | collective-permute-start | bytes 21848 | tf_op jit(solution)/shard_map/ppermute | solution.py:22
  44.0 24.3 %collective-permute-start.7 = (f32[2,7,130,1]{2,1,3,0:T(8,128)}, f32[2,7,130,1]{2,1,3,0:T(8,128)}, u32[]{:S(2)}, u32[]{:S(2)}) collective-permute-start(f32[2,7,130,1]{2,1,3,0:T(8,128)} %get-tuple-element.38), channel_id=1, source_target_pairs={{1,0},{2,1},{3,2},{4,3},{5,4},{6,5},{7,6},{9,8},{10,9},{11,10},{12... | collective-permute-start | bytes 21848 | tf_op jit(solution)/shard_map/ppermute | solution.py:23
  73.6 88.9 %copy-start.1 = (f32[2,7,128,128]{2,1,3,0:T(8,128)}, f32[2,7,128,128]{2,1,3,0:T(8,128)S(1)}, u32[]{:S(2)}) copy-start(f32[2,7,128,128]{2,1,3,0:T(8,128)S(1)} %get-tuple-element.25) | copy-start | bytes 2752516
  76.5 3.8 %collective-permute-start.8 = (f32[2,7,1,128]{3,1,2,0:T(8,128)S(1)}, f32[2,7,1,128]{3,1,2,0:T(8,128)S(1)}, u32[]{:S(2)}, u32[]{:S(2)}) collective-permute-start(f32[2,7,1,128]{3,1,2,0:T(8,128)S(1)} %copy.140), channel_id=1, source_target_pairs={{0,8},{8,16},{16,24},{1,9},{9,17},{17,25},{2,10},{10,18},{18,26},{... | collective-permute-start | bytes 21512 | tf_op jit(solution)/shard_map/ppermute | solution.py:22
  79.0 3.1 %collective-permute-start.9 = (f32[2,7,1,128]{3,1,2,0:T(8,128)S(1)}, f32[2,7,1,128]{3,1,2,0:T(8,128)S(1)}, u32[]{:S(2)}, u32[]{:S(2)}) collective-permute-start(f32[2,7,1,128]{3,1,2,0:T(8,128)S(1)} %copy.142), channel_id=1, source_target_pairs={{8,0},{16,8},{24,16},{9,1},{17,9},{25,17},{10,2},{18,10},{26,18},{... | collective-permute-start | bytes 21512 | tf_op jit(solution)/shard_map/ppermute | solution.py:23
  83.4 6.9 %copy-start.5 = (f32[6,128,128]{1,0,2:T(8,128)S(1)}, f32[6,128,128]{1,0,2:T(8,128)}, u32[]{:S(2)}) copy-start(f32[6,128,128]{1,0,2:T(8,128)} %copy-done.4) | copy-start | bytes 1179652
  83.4 11.2 %copy-start.23 = (f32[2,7,1,128]{2,1,3,0:T(8,128)S(1)}, f32[2,7,1,128]{2,1,3,0:T(8,128)}, u32[]{:S(2)}) copy-start(f32[2,7,1,128]{2,1,3,0:T(8,128)} %copy.143) | copy-start | bytes 21508
  84.4 6.1 %collective-permute-start.10 = (f32[2,7,130,1]{2,1,3,0:T(8,128)S(1)}, f32[2,7,130,1]{2,1,3,0:T(8,128)S(1)}, u32[]{:S(2)}, u32[]{:S(2)}) collective-permute-start(f32[2,7,130,1]{2,1,3,0:T(8,128)S(1)} %get-tuple-element.35), channel_id=1, source_target_pairs={{0,1},{1,2},{2,3},{3,4},{4,5},{5,6},{6,7},{8,9},{9,10},{10,11},{11... | collective-permute-start | bytes 21848 | tf_op jit(solution)/shard_map/ppermute | solution.py:22
  88.7 6.0 %copy-start.7 = (f32[7,128,128]{1,0,2:T(8,128)S(1)}, f32[7,128,128]{1,0,2:T(8,128)}, u32[]{:S(2)}) copy-start(f32[7,128,128]{1,0,2:T(8,128)} %copy.119) | copy-start | bytes 1376260
  88.7 6.0 %copy-start.10 = (f32[7,128,128]{1,0,2:T(8,128)S(1)}, f32[7,128,128]{1,0,2:T(8,128)}, u32[]{:S(2)}) copy-start(f32[7,128,128]{1,0,2:T(8,128)} %copy.124) | copy-start | bytes 1376260
  88.7 5.9 %copy-start.13 = (f32[7,128,128]{1,0,2:T(8,128)S(1)}, f32[7,128,128]{1,0,2:T(8,128)}, u32[]{:S(2)}) copy-start(f32[7,128,128]{1,0,2:T(8,128)} %copy.129) | copy-start | bytes 1376260
  88.7 5.9 %collective-permute-start.11 = (f32[2,7,130,1]{2,1,3,0:T(8,128)S(1)}, f32[2,7,130,1]{2,1,3,0:T(8,128)S(1)}, u32[]{:S(2)}, u32[]{:S(2)}) collective-permute-start(f32[2,7,130,1]{2,1,3,0:T(8,128)S(1)} %get-tuple-element.36), channel_id=1, source_target_pairs={{1,0},{2,1},{3,2},{4,3},{5,4},{6,5},{7,6},{9,8},{10,9},{11,10},{12... | collective-permute-start | bytes 21848 | tf_op jit(solution)/shard_map/ppermute | solution.py:23
  143.3 4.3 %collective-permute-start.12 = (f32[2,7,1,128]{3,1,2,0:T(8,128)S(1)}, f32[2,7,1,128]{3,1,2,0:T(8,128)S(1)}, u32[]{:S(2)}, u32[]{:S(2)}) collective-permute-start(f32[2,7,1,128]{3,1,2,0:T(8,128)S(1)} %copy.147), channel_id=1, source_target_pairs={{0,8},{8,16},{16,24},{1,9},{9,17},{17,25},{2,10},{10,18},{18,26},{... | collective-permute-start | bytes 21512 | tf_op jit(solution)/shard_map/ppermute | solution.py:22
  146.1 5.6 %collective-permute-start.13 = (f32[2,7,1,128]{3,1,2,0:T(8,128)S(1)}, f32[2,7,1,128]{3,1,2,0:T(8,128)S(1)}, u32[]{:S(2)}, u32[]{:S(2)}) collective-permute-start(f32[2,7,1,128]{3,1,2,0:T(8,128)S(1)} %copy.149), channel_id=1, source_target_pairs={{8,0},{16,8},{24,16},{9,1},{17,9},{25,17},{10,2},{18,10},{26,18},{... | collective-permute-start | bytes 21512 | tf_op jit(solution)/shard_map/ppermute | solution.py:23
  153.1 9.4 %copy-start.27 = (f32[2,7,1,128]{2,1,3,0:T(8,128)S(1)}, f32[2,7,1,128]{2,1,3,0:T(8,128)}, u32[]{:S(2)}) copy-start(f32[2,7,1,128]{2,1,3,0:T(8,128)} %copy.148) | copy-start | bytes 21508
  153.1 9.4 %copy-start.28 = (f32[2,7,1,128]{2,1,3,0:T(8,128)S(1)}, f32[2,7,1,128]{2,1,3,0:T(8,128)}, u32[]{:S(2)}) copy-start(f32[2,7,1,128]{2,1,3,0:T(8,128)} %copy.150) | copy-start | bytes 21508
  154.1 4.3 %collective-permute-start.14 = (f32[2,7,130,1]{2,1,3,0:T(8,128)S(1)}, f32[2,7,130,1]{2,1,3,0:T(8,128)S(1)}, u32[]{:S(2)}, u32[]{:S(2)}) collective-permute-start(f32[2,7,130,1]{2,1,3,0:T(8,128)S(1)} %get-tuple-element.33), channel_id=1, source_target_pairs={{0,1},{1,2},{2,3},{3,4},{4,5},{5,6},{6,7},{8,9},{9,10},{10,11},{11... | collective-permute-start | bytes 21848 | tf_op jit(solution)/shard_map/ppermute | solution.py:22
  156.5 6.0 %copy-start.3 = (f32[2,7,128,128]{2,1,3,0:T(8,128)S(1)}, f32[2,7,128,128]{2,1,3,0:T(8,128)}, u32[]{:S(2)}) copy-start(f32[2,7,128,128]{2,1,3,0:T(8,128)} %get-tuple-element.23) | copy-start | bytes 2752516
  156.6 6.0 %copy-start.8 = (f32[7,128,128]{1,0,2:T(8,128)S(1)}, f32[7,128,128]{1,0,2:T(8,128)}, u32[]{:S(2)}) copy-start(f32[7,128,128]{1,0,2:T(8,128)} %copy.119) | copy-start | bytes 1376260
  156.6 6.0 %copy-start.11 = (f32[7,128,128]{1,0,2:T(8,128)S(1)}, f32[7,128,128]{1,0,2:T(8,128)}, u32[]{:S(2)}) copy-start(f32[7,128,128]{1,0,2:T(8,128)} %copy.124) | copy-start | bytes 1376260
  156.6 6.0 %copy-start.14 = (f32[7,128,128]{1,0,2:T(8,128)S(1)}, f32[7,128,128]{1,0,2:T(8,128)}, u32[]{:S(2)}) copy-start(f32[7,128,128]{1,0,2:T(8,128)} %copy.129) | copy-start | bytes 1376260
  156.6 6.0 %copy-start.17 = (f32[7,128,128]{1,0,2:T(8,128)S(1)}, f32[7,128,128]{1,0,2:T(8,128)}, u32[]{:S(2)}) copy-start(f32[7,128,128]{1,0,2:T(8,128)} %copy.134) | copy-start | bytes 1376260
  156.6 6.0 %copy-start.20 = (f32[7,128,128]{1,0,2:T(8,128)S(1)}, f32[7,128,128]{1,0,2:T(8,128)}, u32[]{:S(2)}) copy-start(f32[7,128,128]{1,0,2:T(8,128)} %copy.117) | copy-start | bytes 1376260
  156.6 5.9 %collective-permute-start.15 = (f32[2,7,130,1]{2,1,3,0:T(8,128)S(1)}, f32[2,7,130,1]{2,1,3,0:T(8,128)S(1)}, u32[]{:S(2)}, u32[]{:S(2)}) collective-permute-start(f32[2,7,130,1]{2,1,3,0:T(8,128)S(1)} %get-tuple-element.34), channel_id=1, source_target_pairs={{1,0},{2,1},{3,2},{4,3},{5,4},{6,5},{7,6},{9,8},{10,9},{11,10},{12... | collective-permute-start | bytes 21848 | tf_op jit(solution)/shard_map/ppermute | solution.py:23
  215.9 7.9 %collective-permute-start.17 = (f32[2,7,1,128]{3,1,2,0:T(8,128)S(1)}, f32[2,7,1,128]{3,1,2,0:T(8,128)S(1)}, u32[]{:S(2)}, u32[]{:S(2)}) collective-permute-start(f32[2,7,1,128]{3,1,2,0:T(8,128)S(1)} %copy.155), channel_id=1, source_target_pairs={{8,0},{16,8},{24,16},{9,1},{17,9},{25,17},{10,2},{18,10},{26,18},{... | collective-permute-start | bytes 21512 | tf_op jit(solution)/shard_map/ppermute | solution.py:23
  217.2 5.2 %collective-permute-start.16 = (f32[2,7,1,128]{3,1,2,0:T(8,128)S(1)}, f32[2,7,1,128]{3,1,2,0:T(8,128)S(1)}, u32[]{:S(2)}, u32[]{:S(2)}) collective-permute-start(f32[2,7,1,128]{3,1,2,0:T(8,128)S(1)} %copy.153), channel_id=1, source_target_pairs={{0,8},{8,16},{16,24},{1,9},{9,17},{17,25},{2,10},{10,18},{18,26},{... | collective-permute-start | bytes 21512 | tf_op jit(solution)/shard_map/ppermute | solution.py:22
  225.1 6.5 %copy-start.2 = (f32[7,128,128]{1,0,2:T(8,128)S(1)}, f32[7,128,128]{1,0,2:T(8,128)}, u32[]{:S(2)}) copy-start(f32[7,128,128]{1,0,2:T(8,128)} %copy.139) | copy-start | bytes 1376260
  225.1 6.5 %copy-start.24 = (f32[2,7,128,128]{2,1,3,0:T(8,128)S(1)}, f32[2,7,128,128]{2,1,3,0:T(8,128)}, u32[]{:S(2)}) copy-start(f32[2,7,128,128]{2,1,3,0:T(8,128)} %get-tuple-element.18) | copy-start | bytes 2752516
  225.1 10.8 %copy-start.18 = (f32[7,128,128]{1,0,2:T(8,128)S(1)}, f32[7,128,128]{1,0,2:T(8,128)}, u32[]{:S(2)}) copy-start(f32[7,128,128]{1,0,2:T(8,128)} %copy.134) | copy-start | bytes 1376260
  225.1 10.8 %copy-start.21 = (f32[7,128,128]{1,0,2:T(8,128)S(1)}, f32[7,128,128]{1,0,2:T(8,128)}, u32[]{:S(2)}) copy-start(f32[7,128,128]{1,0,2:T(8,128)} %copy.117) | copy-start | bytes 1376260
  226.1 5.8 %collective-permute-start.18 = (f32[2,7,130,1]{2,1,3,0:T(8,128)S(1)}, f32[2,7,130,1]{2,1,3,0:T(8,128)S(1)}, u32[]{:S(2)}, u32[]{:S(2)}) collective-permute-start(f32[2,7,130,1]{2,1,3,0:T(8,128)S(1)} %get-tuple-element.31), channel_id=1, source_target_pairs={{0,1},{1,2},{2,3},{3,4},{4,5},{5,6},{6,7},{8,9},{9,10},{10,11},{11... | collective-permute-start | bytes 21848 | tf_op jit(solution)/shard_map/ppermute | solution.py:22
  230.3 5.6 %collective-permute-start.19 = (f32[2,7,130,1]{2,1,3,0:T(8,128)S(1)}, f32[2,7,130,1]{2,1,3,0:T(8,128)S(1)}, u32[]{:S(2)}, u32[]{:S(2)}) collective-permute-start(f32[2,7,130,1]{2,1,3,0:T(8,128)S(1)} %get-tuple-element.32), channel_id=1, source_target_pairs={{1,0},{2,1},{3,2},{4,3},{5,4},{6,5},{7,6},{9,8},{10,9},{11,10},{12... | collective-permute-start | bytes 21848 | tf_op jit(solution)/shard_map/ppermute | solution.py:23
  (17 other events, 51.6 us)
where the time goes:
time: 285 us; the launch traced here: 284 us
  blocking collectives  123 us (43%)
  starting transfers between devices  48.3 us (17%)
  local copies, waits for them, and re-layouts  47.9 us (17%)
  other arithmetic  35.5 us (12%)
  waiting for transfers between devices  28.2 us (10%)
    psum x3, blocking collectives, both_sums(): lax.psum((core_sum(residual, scaled), core_sum(scaled, image)), ('gx', 'g...  123 us
    ppermute x10, starting transfers between devices, extended_2(): before = lax.ppermute(last, axis, up)  34.7 us
    ppermute x10, waiting for transfers between devices, extended_2(): after = lax.ppermute(leading, axis, down)  16.7 us
    ppermute x10, starting transfers between devices, extended_2(): after = lax.ppermute(leading, axis, down)  13.6 us
    ppermute x10, waiting for transfers between devices, extended_2(): before = lax.ppermute(last, axis, up)  11.5 us
    reduce_sum x4, other arithmetic, core_sum(): return jnp.sum(first * second, axis=(1, 2, 3))  10.6 us
    div x3, other arithmetic, per_device(): scaled = residual / diagonal  10.3 us
    slice x7, local copies, waits for them, and re-layouts, extended_2(): last = lax.slice_in_dim(x, length - width, length, axis=dim)  10.2 us
  transfers between devices with their start and end apart: 20, of which 7 were waited for; matrix products, arithmetic and copies ran while one was open for 13% of the time, Pallas kernels for 0%

commit v1 on v0

--- a/solution.py
+++ b/solution.py
@@ -10,6 +10,11 @@
 TIER_HEAT = 0.05
 CHANNEL_HEAT = 0.2
 VERTICAL = 4.0
+
+
+def axis_by_axis(array, inner_axis, outer_axis):
+    inner = lax.psum(array, inner_axis)
+    return lax.psum(inner, outer_axis)
 
 
 def extended_2(x, sides, width):
@@ -95,7 +100,7 @@
 
 
 def both_sums(residual, scaled, image):
-    return lax.psum((core_sum(residual, scaled), core_sum(scaled, image)), ("gx", "gy"))
+    return axis_by_axis((core_sum(residual, scaled), core_sum(scaled, image)), "gy", "gx")
 
 
 def per_device(previous, dissipated, material, coolant):

time: 285 us -> 233 us (0.82)
  blocking collectives: 123 us -> 72.6 us
    psum x3 -> x6, blocking collectives: 123 us -> 72.6 us  [the longest x3 54.9 us: axis_by_axis(): inner = lax.psum(array, inner_axis)]
  transfers between devices with their start and end apart: 20 -> 20, of which waited for: 7 -> 7; matrix products, arithmetic and copies ran while one was open for 13% -> 16% of each run, Pallas kernels for 0% -> 0%
where the time goes in v1:
time: 233 us; the launch traced here: 232 us
  blocking collectives  72.6 us (31%)
  local copies, waits for them, and re-layouts  48 us (21%)
  starting transfers between devices  47.5 us (20%)
  other arithmetic  35.5 us (15%)
  waiting for transfers between devices  27.1 us (12%)
    psum x3, blocking collectives, axis_by_axis(): inner = lax.psum(array, inner_axis)  54.9 us
    ppermute x10, starting transfers between devices, extended_2(): before = lax.ppermute(last, axis, up)  33.9 us
    psum x3, blocking collectives, axis_by_axis(): return lax.psum(inner, outer_axis)  17.7 us
    ppermute x10, waiting for transfers between devices, extended_2(): after = lax.ppermute(leading, axis, down)  15.7 us
    ppermute x10, starting transfers between devices, extended_2(): after = lax.ppermute(leading, axis, down)  13.6 us
    ppermute x10, waiting for transfers between devices, extended_2(): before = lax.ppermute(last, axis, up)  11.5 us
    reduce_sum x4, other arithmetic, core_sum(): return jnp.sum(first * second, axis=(1, 2, 3))  10.6 us
    slice x7, local copies, waits for them, and re-layouts, extended_2(): last = lax.slice_in_dim(x, length - width, length, axis=dim)  10.2 us
  transfers between devices with their start and end apart: 20, of which 7 were waited for; matrix products, arithmetic and copies ran while one was open for 16% of the time, Pallas kernels for 0%

profile of v1, /device:TPU:0, one launch (start us, length us, event | category | flops | bytes accessed | tf_op | source)
XLA Modules:
  0.0 231.6 jit_solution(13868929208807221151)
XLA Ops:
  3.3 3.7 %collective-permute-start.1 = (f32[2,7,1,128]{3,1,2,0:T(8,128)}, f32[2,7,1,128]{3,1,2,0:T(8,128)}, u32[]{:S(2)}, u32[]{:S(2)}) collective-permute-start(f32[2,7,1,128]{3,1,2,0:T(8,128)} %copy.160), channel_id=1, source_target_pairs={{0,8},{8,16},{16,24},{1,9},{9,17},{17,25},{2,10},{10,18},{18,26},{... | collective-permute-start | bytes 21512 | tf_op jit(solution)/shard_map/ppermute | solution.py:27
  10.3 4.6 %collective-permute-start = (f32[7,1,128]{2,1,0:T(1,128)}, f32[7,1,128]{2,1,0:T(1,128)S(1)}, u32[]{:S(2)}, u32[]{:S(2)}) collective-permute-start(f32[7,1,128]{2,1,0:T(1,128)} %get-tuple-element.61), channel_id=1, source_target_pairs={{0,8},{8,16},{16,24},{1,9},{9,17},{17,25},{2,10},{10,18},{18,26},{... | collective-permute-start | bytes 10760 | tf_op jit(solution)/shard_map/ppermute | solution.py:27
  27.0 2.5 %stack.15 = f32[2,7,128,128]{2,1,3,0:T(8,128)} concatenate(f32[2,1,128,128]{2,1,3,0:T(1,128)S(1)} %copy.113, f32[2,1,128,128]{2,1,3,0:T(1,128)S(1)} %broadcast.72, f32[2,1,128,128]{2,1,3,0:T(1,128)S(1)} %copy.114, f32[2,1,128,128]{2,1,3,0:T(1,128)S(1)} %broadcast.72, f32[2,1,128,128]{2,1,3,0:T(1,128)S(1)} %copy.115, f32[2,1,128,128]{2,1,3,0:T(1,128)S(1)} %broadcast.72, ...), dimensions={1} | concatenate | bytes 1835008 | tf_op jit(solution)/shard_map/stack | solution.py:53
  32.4 5.3 %collective-permute-start.4 = (f32[7,130,1]{2,1,0:T(8,128)}, f32[7,130,1]{2,1,0:T(8,128)}, u32[]{:S(2)}, u32[]{:S(2)}) collective-permute-start(f32[7,130,1]{2,1,0:T(8,128)} %get-tuple-element.58), channel_id=1, source_target_pairs={{0,1},{1,2},{2,3},{3,4},{4,5},{5,6},{6,7},{8,9},{9,10},{10,11},{11... | collective-permute-start | bytes 10928 | tf_op jit(solution)/shard_map/ppermute | solution.py:27
  40.3 3.6 %collective-permute-start.5 = (f32[2,7,130,1]{2,1,3,0:T(8,128)}, f32[2,7,130,1]{2,1,3,0:T(8,128)S(1)}, u32[]{:S(2)}, u32[]{:S(2)}) collective-permute-start(f32[2,7,130,1]{2,1,3,0:T(8,128)} %get-tuple-element.43), channel_id=1, source_target_pairs={{0,1},{1,2},{2,3},{3,4},{4,5},{5,6},{6,7},{8,9},{9,10},{10,11},{11... | collective-permute-start | bytes 21848 | tf_op jit(solution)/shard_map/ppermute | solution.py:27
  46.6 11.4 %collective-permute-done.4 = f32[7,130,1]{2,1,0:T(8,128)} collective-permute-done((f32[7,130,1]{2,1,0:T(8,128)}, f32[7,130,1]{2,1,0:T(8,128)}, u32[]{:S(2)}, u32[]{:S(2)}) %collective-permute-start.4) | collective-permute-done | bytes 3672 | tf_op jit(solution)/shard_map/ppermute | solution.py:27
  58.0 3.0 %add_add_fusion = (f32[7,128,128]{2,1,0:T(8,128)}, f32[7,128,128]{2,1,0:T(8,128)}, f32[7,128,128]{2,1,0:T(8,128)S(1)}, f32[7,128,128]{2,1,0:T(8,128)S(1)}, f32[7...) fusion(f32[6,128,128]{2,1,0:T(8,128)S(1)} %sqrt_multiply_fusion, f32[7,128,128]{2,1,0:T(8,128)S(1)} %copy-done.33, ...), kind=kLoop, calls=%fused_computation.123 | loop fusion | flops 2179072 | bytes 4077708 | tf_op jit(solution)/shard_map/add | solution.py:95
  61.0 2.1 copy.139
  68.3 5.3 %broadcast_divide_fusion.2 = (f32[2,7,128,128]{2,1,3,0:T(8,128)S(1)}, f32[2,7,128,128]{2,1,3,0:T(8,128)S(1)}) fusion(f32[7,128,128]{1,0,2:T(8,128)} %copy.139, f32[2,6,128,128]{2,1,3,0:T(8,128)} %fusion.44, f32[2,7,128,128]{2,1,3,0:T(8,128)S(1)} %copy.146, f32[2,7,130,1]{2,1,3,0:T(8,128)} %collective-permute-done.7, f32[2,7,1,128]{2,1,3,0:T(8,128)} %copy-done.26, ...), kind=kLoop, calls=%fused_computation.105 | loop fusion | flops 6193152 | bytes 7237884 | tf_op jit(solution)/shard_map/div | solution.py:127
  73.6 1.3 fusion.77
  74.9 1.6 copy.140
  76.5 2.1 collective-permute-start.8
  80.3 1.4 copy.141
  82.0 1.4 copy.143
  84.3 4.3 %collective-permute-start.10 = (f32[2,7,130,1]{2,1,3,0:T(8,128)S(1)}, f32[2,7,130,1]{2,1,3,0:T(8,128)S(1)}, u32[]{:S(2)}, u32[]{:S(2)}) collective-permute-start(f32[2,7,130,1]{2,1,3,0:T(8,128)S(1)} %get-tuple-element.41), channel_id=1, source_target_pairs={{0,1},{1,2},{2,3},{3,4},{4,5},{5,6},{6,7},{8,9},{9,10},{10,11},{11... | collective-permute-start | bytes 21848 | tf_op jit(solution)/shard_map/ppermute | solution.py:27
  88.7 1.6 collective-permute-start.11
  90.4 4.2 %collective-permute-done.11 = f32[2,7,130,1]{2,1,3,0:T(8,128)S(1)} collective-permute-done((f32[2,7,130,1]{2,1,3,0:T(8,128)S(1)}, f32[2,7,130,1]{2,1,3,0:T(8,128)S(1)}, u32[]{:S(2)}, u32[]{:S(2)}) %collective-permute-start.11) | collective-permute-done | bytes 7312 | tf_op jit(solution)/shard_map/ppermute | solution.py:28
  94.6 3.1 %multiply_reduce_fusion.3 = (f32[2]{0:T(128)S(1)}, f32[2]{0:T(128)S(1)}, f32[2,7,128,128]{2,1,3,0:T(8,128)}) fusion(f32[2,7,128,128]{2,1,3,0:T(8,128)S(1)} %get-tuple-element.30, f32[2,7,128,128]{2,1,3,0:T(8,128)S(1)} %get-tuple-element.31, f32[2,6,128,128]{2,1,3,0:T(8,128)S(1)} %fusion.30, f32[2,7,130,1]{2,1,3,0:T(8,128)S(1)} %collective-permute-done.11, ...), kind=kLoop, calls=%fused_computation.101 | loop fusion | flops 6193148 | bytes 5861616 | tf_op jit(solution)/shard_map/reduce_sum | solution.py:99
  97.7 18.8 %all-reduce.12 = (f32[2]{0:T(128)S(1)}, f32[2]{0:T(128)S(1)}) all-reduce(f32[2]{0:T(128)S(1)} %get-tuple-element.8, f32[2]{0:T(128)S(1)} %get-tuple-element.7), channel_id=1, replica_groups=mesh['gx'=4,'gy'=8] {'gy'}, use_global_device_ids=true, to_apply=%region_1.2 | all-reduce | flops 4 | bytes 32 | tf_op jit(solution)/shard_map/psum | solution.py:16
  116.5 5.6 %all-reduce.15 = (f32[2]{0:T(128)S(1)}, f32[2]{0:T(128)S(1)}) all-reduce(f32[2]{0:T(128)S(1)} %get-tuple-element.13, f32[2]{0:T(128)S(1)} %get-tuple-element.14), channel_id=1, replica_groups=mesh['gx'=4,'gy'=8] {'gx'}, use_global_device_ids=true, to_apply=%region_2.3 | all-reduce | flops 4 | bytes 32 | tf_op jit(solution)/shard_map/psum | solution.py:17
  122.2 1.6 broadcast_divide_fusion.1
  123.8 1.7 fusion.76
  125.5 1.6 copy.147
  127.0 2.0 collective-permute-start.12
  129.0 1.6 copy.149
  131.9 1.4 copy.148
  133.3 1.9 collective-permute-done.13
  135.1 1.4 copy.150
  137.5 2.2 collective-permute-start.14
  139.8 1.7 collective-permute-start.15
  141.7 4.0 %collective-permute-done.15 = f32[2,7,130,1]{2,1,3,0:T(8,128)S(1)} collective-permute-done((f32[2,7,130,1]{2,1,3,0:T(8,128)S(1)}, f32[2,7,130,1]{2,1,3,0:T(8,128)S(1)}, u32[]{:S(2)}, u32[]{:S(2)}) %collective-permute-start.15) | collective-permute-done | bytes 7312 | tf_op jit(solution)/shard_map/ppermute | solution.py:28
  145.7 3.2 %multiply_reduce_fusion.1 = (f32[2]{0:T(128)S(1)}, f32[2]{0:T(128)S(1)}, f32[2,7,128,128]{2,1,3,0:T(8,128)}) fusion(f32[2,7,128,128]{2,1,3,0:T(8,128)S(1)} %broadcast_divide_fusion.1, f32[2,7,128,128]{2,1,3,0:T(8,128)S(1)} %get-tuple-element.31, f32[2,7,128,128]{2,1,3,0:T(8,128)S(1)} %copy-done.3, f32[2]{0:T(128)S(1)} %div.43, ...), kind=kLoop, calls=%fused_computation.98 | loop fusion | flops 6651900 | bytes 6779128 | tf_op jit(solution)/shard_map/reduce_sum | solution.py:99
  148.9 18.0 %all-reduce.11 = (f32[2]{0:T(128)S(1)}, f32[2]{0:T(128)S(1)}) all-reduce(f32[2]{0:T(128)S(1)} %get-tuple-element.6, f32[2]{0:T(128)S(1)} %get-tuple-element.5), channel_id=1, replica_groups=mesh['gx'=4,'gy'=8] {'gy'}, use_global_device_ids=true, to_apply=%region_7.8 | all-reduce | flops 4 | bytes 32 | tf_op jit(solution)/shard_map/psum | solution.py:16
  166.9 6.0 %all-reduce.14 = (f32[2]{0:T(128)S(1)}, f32[2]{0:T(128)S(1)}) all-reduce(f32[2]{0:T(128)S(1)} %get-tuple-element.11, f32[2]{0:T(128)S(1)} %get-tuple-element.12), channel_id=1, replica_groups=mesh['gx'=4,'gy'=8] {'gx'}, use_global_device_ids=true, to_apply=%region_8.9 | all-reduce | flops 4 | bytes 32 | tf_op jit(solution)/shard_map/psum | solution.py:17
  172.9 3.3 %broadcast_divide_fusion = (f32[2,7,128,128]{2,1,3,0:T(8,128)S(1)}, f32[2,7,128,128]{2,1,3,0:T(8,128)}) fusion(f32[7,128,128]{1,0,2:T(8,128)} %copy.139, f32[2,7,128,128]{2,1,3,0:T(8,128)} %get-tuple-element.28, f32[2,7,128,128]{2,1,3,0:T(8,128)} %get-tuple-element.29, f32[2]{0:T(128)S(1)} %get-tuple-element.27, f32[2]{0:T(128)S(1)} %get-tuple-element.25, ...), kind=kLoop, calls=%fused_computation.103 | loop fusion | flops 1605632 | bytes 5046296 | tf_op jit(solution)/shard_map/div | solution.py:138
  176.2 1.7 fusion.75
  177.9 1.6 copy.153
  179.5 1.6 copy.155
  182.3 3.0 %collective-permute-start.16 = (f32[2,7,1,128]{3,1,2,0:T(8,128)S(1)}, f32[2,7,1,128]{3,1,2,0:T(8,128)S(1)}, u32[]{:S(2)}, u32[]{:S(2)}) collective-permute-start(f32[2,7,1,128]{3,1,2,0:T(8,128)S(1)} %copy.153), channel_id=1, source_target_pairs={{0,8},{8,16},{16,24},{1,9},{9,17},{17,25},{2,10},{10,18},{18,26},{... | collective-permute-start | bytes 21512 | tf_op jit(solution)/shard_map/ppermute | solution.py:27
  185.4 2.2 fusion
  187.5 1.4 copy.154
  188.9 1.4 copy.156
  191.3 3.0 %collective-permute-start.18 = (f32[2,7,130,1]{2,1,3,0:T(8,128)S(1)}, f32[2,7,130,1]{2,1,3,0:T(8,128)S(1)}, u32[]{:S(2)}, u32[]{:S(2)}) collective-permute-start(f32[2,7,130,1]{2,1,3,0:T(8,128)S(1)} %get-tuple-element.37), channel_id=1, source_target_pairs={{0,1},{1,2},{2,3},{3,4},{4,5},{5,6},{6,7},{8,9},{9,10},{10,11},{11... | collective-permute-start | bytes 21848 | tf_op jit(solution)/shard_map/ppermute | solution.py:27
  195.9 4.0 %collective-permute-done.19 = f32[2,7,130,1]{2,1,3,0:T(8,128)S(1)} collective-permute-done((f32[2,7,130,1]{2,1,3,0:T(8,128)S(1)}, f32[2,7,130,1]{2,1,3,0:T(8,128)S(1)}, u32[]{:S(2)}, u32[]{:S(2)}) %collective-permute-start.19) | collective-permute-done | bytes 7312 | tf_op jit(solution)/shard_map/ppermute | solution.py:28
  199.9 4.1 %fusion.7 = f32[2]{0:T(128)S(1)} fusion(f32[2,7,128,128]{2,1,3,0:T(8,128)S(1)} %get-tuple-element.23, f32[2,7,130,1]{2,1,3,0:T(8,128)S(1)} %collective-permute-done.19, f32[2,7,1,128]{2,1,3,0:T(8,128)} %copy.156, f32[2,7,1,128]{2,1,3,0:T(8,128)} %copy.154, f32[2,7,130,1]{2,1,3,0:T(8,128)S(1)} %collective-permute-done.18, f32[2,6,128,128]{2,1,3,0:T(8,128)} %fusion, ...), kind=kLoop, calls=%fused_computation.9 | loop fusion | flops 5734398 | bytes 4026600 | tf_op jit(solution)/shard_map/reduce_sum | solution.py:99
  204.0 18.0 %all-reduce.10 = (f32[2]{0:T(128)S(1)}, f32[2]{0:T(128)S(1)}) all-reduce(f32[2]{0:T(128)S(1)} %multiply_reduce_fusion, f32[2]{0:T(128)S(1)} %fusion.7), channel_id=1, replica_groups=mesh['gx'=4,'gy'=8] {'gy'}, use_global_device_ids=true, to_apply=%region_13.14 | all-reduce | flops 4 | bytes 32 | tf_op jit(solution)/shard_map/psum | solution.py:16
  222.1 6.1 %all-reduce.13 = (f32[2]{0:T(128)S(1)}, f32[2]{0:T(128)S(1)}) all-reduce(f32[2]{0:T(128)S(1)} %get-tuple-element.9, f32[2]{0:T(128)S(1)} %get-tuple-element.10), channel_id=1, replica_groups=mesh['gx'=4,'gy'=8] {'gx'}, use_global_device_ids=true, to_apply=%region_14.15 | all-reduce | flops 4 | bytes 32 | tf_op jit(solution)/shard_map/psum | solution.py:17
  228.2 2.1 multiply_add_fusion
  (168 shorter events, 42.5 us)
Async XLA Ops:
  1.5 37.4 %collective-permute-start.3 = (f32[2,7,1,128]{3,1,2,0:T(8,128)}, f32[2,7,1,128]{3,1,2,0:T(8,128)S(1)}, u32[]{:S(2)}, u32[]{:S(2)}) collective-permute-start(f32[2,7,1,128]{3,1,2,0:T(8,128)} %copy.161), channel_id=1, source_target_pairs={{8,0},{16,8},{24,16},{9,1},{17,9},{25,17},{10,2},{18,10},{26,18},{... | collective-permute-start | bytes 21512 | tf_op jit(solution)/shard_map/ppermute | solution.py:28
  3.3 34.4 %collective-permute-start.1 = (f32[2,7,1,128]{3,1,2,0:T(8,128)}, f32[2,7,1,128]{3,1,2,0:T(8,128)}, u32[]{:S(2)}, u32[]{:S(2)}) collective-permute-start(f32[2,7,1,128]{3,1,2,0:T(8,128)} %copy.160), channel_id=1, source_target_pairs={{0,8},{8,16},{16,24},{1,9},{9,17},{17,25},{2,10},{10,18},{18,26},{... | collective-permute-start | bytes 21512 | tf_op jit(solution)/shard_map/ppermute | solution.py:27
  8.1 7.4 %copy-start.32 = (f32[2,7,128,128]{3,2,1,0:T(8,128)S(1)}, f32[2,7,128,128]{3,2,1,0:T(8,128)}, u32[]{:S(2)}) copy-start(f32[2,7,128,128]{3,2,1,0:T(8,128)} %param.5) | copy-start | bytes 2752516
  8.4 6.5 %copy-start.34 = (f32[6,128,128]{2,1,0:T(8,128)}, f32[6,128,128]{2,1,0:T(8,128)S(1)}, u32[]{:S(2)}) copy-start(f32[6,128,128]{2,1,0:T(8,128)S(1)} %get-tuple-element.64) | copy-start | bytes 1179652
  8.4 6.5 %copy-start.36 = (f32[6,128,128]{2,1,0:T(8,128)}, f32[6,128,128]{2,1,0:T(8,128)S(1)}, u32[]{:S(2)}) copy-start(f32[6,128,128]{2,1,0:T(8,128)S(1)} %get-tuple-element.63) | copy-start | bytes 1179652
  8.4 21.0 %copy-start.29 = (f32[7,128,128]{2,1,0:T(8,128)}, f32[7,128,128]{2,1,0:T(8,128)S(1)}, u32[]{:S(2)}) copy-start(f32[7,128,128]{2,1,0:T(8,128)S(1)} %get-tuple-element.62) | copy-start | bytes 1376260
  9.0 20.4 %collective-permute-start.2 = (f32[7,1,128]{2,1,0:T(1,128)}, f32[7,1,128]{2,1,0:T(1,128)S(1)}, u32[]{:S(2)}, u32[]{:S(2)}) collective-permute-start(f32[7,1,128]{2,1,0:T(1,128)} %get-tuple-element.60), channel_id=1, source_target_pairs={{8,0},{16,8},{24,16},{9,1},{17,9},{25,17},{10,2},{18,10},{26,18},{... | collective-permute-start | bytes 10760 | tf_op jit(solution)/shard_map/ppermute | solution.py:28
  10.3 19.1 %collective-permute-start = (f32[7,1,128]{2,1,0:T(1,128)}, f32[7,1,128]{2,1,0:T(1,128)S(1)}, u32[]{:S(2)}, u32[]{:S(2)}) collective-permute-start(f32[7,1,128]{2,1,0:T(1,128)} %get-tuple-element.61), channel_id=1, source_target_pairs={{0,8},{8,16},{16,24},{1,9},{9,17},{17,25},{2,10},{10,18},{18,26},{... | collective-permute-start | bytes 10760 | tf_op jit(solution)/shard_map/ppermute | solution.py:27
  16.0 52.3 %copy-start = (f32[2,7,128,128]{2,1,3,0:T(8,128)}, f32[2,7,128,128]{2,1,3,0:T(8,128)S(1)}, u32[]{:S(2)}) copy-start(f32[2,7,128,128]{2,1,3,0:T(8,128)S(1)} %copy.146) | copy-start | bytes 2752516
  31.1 15.4 %collective-permute-start.6 = (f32[7,130,1]{2,1,0:T(8,128)}, f32[7,130,1]{2,1,0:T(8,128)}, u32[]{:S(2)}, u32[]{:S(2)}) collective-permute-start(f32[7,130,1]{2,1,0:T(8,128)} %get-tuple-element.57), channel_id=1, source_target_pairs={{1,0},{2,1},{3,2},{4,3},{5,4},{6,5},{7,6},{9,8},{10,9},{11,10},{12... | collective-permute-start | bytes 10928 | tf_op jit(solution)/shard_map/ppermute | solution.py:28
  32.4 25.6 %collective-permute-start.4 = (f32[7,130,1]{2,1,0:T(8,128)}, f32[7,130,1]{2,1,0:T(8,128)}, u32[]{:S(2)}, u32[]{:S(2)}) collective-permute-start(f32[7,130,1]{2,1,0:T(8,128)} %get-tuple-element.58), channel_id=1, source_target_pairs={{0,1},{1,2},{2,3},{3,4},{4,5},{5,6},{6,7},{8,9},{9,10},{10,11},{11... | collective-permute-start | bytes 10928 | tf_op jit(solution)/shard_map/ppermute | solution.py:27
  39.3 18.7 %copy-start.30 = (f32[7,128,128]{2,1,0:T(8,128)S(1)}, f32[7,128,128]{2,1,0:T(8,128)}, u32[]{:S(2)}) copy-start(f32[7,128,128]{2,1,0:T(8,128)} %copy-done.29) | copy-start | bytes 1376260
  39.3 18.7 %copy-start.33 = (f32[7,128,128]{2,1,0:T(8,128)S(1)}, f32[7,128,128]{2,1,0:T(8,128)}, u32[]{:S(2)}) copy-start(f32[7,128,128]{2,1,0:T(8,128)} %constant_dynamic-update-slice_fusion) | copy-start | bytes 1376260
  39.3 18.7 %copy-start.42 = (f32[7,1,128]{2,1,0:T(1,128)S(1)}, f32[7,1,128]{2,1,0:T(1,128)}, u32[]{:S(2)}) copy-start(f32[7,1,128]{2,1,0:T(1,128)} %copy-done.41) | copy-start | bytes 10756
  39.3 18.7 %copy-start.43 = (f32[7]{0:T(128)S(1)}, f32[7]{0:T(128)}, u32[]{:S(2)}) copy-start(f32[7]{0:T(128)} %constant.10.clone) | copy-start | bytes 88
  40.3 17.7 %copy-start.40 = (f32[7,1,128]{2,1,0:T(1,128)S(1)}, f32[7,1,128]{2,1,0:T(1,128)}, u32[]{:S(2)}) copy-start(f32[7,1,128]{2,1,0:T(1,128)} %copy-done.39) | copy-start | bytes 10756
  40.3 28.0 %collective-permute-start.5 = (f32[2,7,130,1]{2,1,3,0:T(8,128)}, f32[2,7,130,1]{2,1,3,0:T(8,128)S(1)}, u32[]{:S(2)}, u32[]{:S(2)}) collective-permute-start(f32[2,7,130,1]{2,1,3,0:T(8,128)} %get-tuple-element.43), channel_id=1, source_target_pairs={{0,1},{1,2},{2,3},{3,4},{4,5},{5,6},{6,7},{8,9},{9,10},{10,11},{11... | collective-permute-start | bytes 21848 | tf_op jit(solution)/shard_map/ppermute | solution.py:27
  44.0 24.3 %collective-permute-start.7 = (f32[2,7,130,1]{2,1,3,0:T(8,128)}, f32[2,7,130,1]{2,1,3,0:T(8,128)}, u32[]{:S(2)}, u32[]{:S(2)}) collective-permute-start(f32[2,7,130,1]{2,1,3,0:T(8,128)} %get-tuple-element.44), channel_id=1, source_target_pairs={{1,0},{2,1},{3,2},{4,3},{5,4},{6,5},{7,6},{9,8},{10,9},{11,10},{12... | collective-permute-start | bytes 21848 | tf_op jit(solution)/shard_map/ppermute | solution.py:28
  73.6 72.1 %copy-start.1 = (f32[2,7,128,128]{2,1,3,0:T(8,128)}, f32[2,7,128,128]{2,1,3,0:T(8,128)S(1)}, u32[]{:S(2)}) copy-start(f32[2,7,128,128]{2,1,3,0:T(8,128)S(1)} %get-tuple-element.31) | copy-start | bytes 2752516
  76.5 3.8 %collective-permute-start.8 = (f32[2,7,1,128]{3,1,2,0:T(8,128)S(1)}, f32[2,7,1,128]{3,1,2,0:T(8,128)S(1)}, u32[]{:S(2)}, u32[]{:S(2)}) collective-permute-start(f32[2,7,1,128]{3,1,2,0:T(8,128)S(1)} %copy.140), channel_id=1, source_target_pairs={{0,8},{8,16},{16,24},{1,9},{9,17},{17,25},{2,10},{10,18},{18,26},{... | collective-permute-start | bytes 21512 | tf_op jit(solution)/shard_map/ppermute | solution.py:27
  78.9 3.1 %collective-permute-start.9 = (f32[2,7,1,128]{3,1,2,0:T(8,128)S(1)}, f32[2,7,1,128]{3,1,2,0:T(8,128)S(1)}, u32[]{:S(2)}, u32[]{:S(2)}) collective-permute-start(f32[2,7,1,128]{3,1,2,0:T(8,128)S(1)} %copy.142), channel_id=1, source_target_pairs={{8,0},{16,8},{24,16},{9,1},{17,9},{25,17},{10,2},{18,10},{26,18},{... | collective-permute-start | bytes 21512 | tf_op jit(solution)/shard_map/ppermute | solution.py:28
  83.4 6.9 %copy-start.5 = (f32[6,128,128]{1,0,2:T(8,128)S(1)}, f32[6,128,128]{1,0,2:T(8,128)}, u32[]{:S(2)}) copy-start(f32[6,128,128]{1,0,2:T(8,128)} %copy-done.4) | copy-start | bytes 1179652
  83.4 11.2 %copy-start.23 = (f32[2,7,1,128]{2,1,3,0:T(8,128)S(1)}, f32[2,7,1,128]{2,1,3,0:T(8,128)}, u32[]{:S(2)}) copy-start(f32[2,7,1,128]{2,1,3,0:T(8,128)} %copy.143) | copy-start | bytes 21508
  84.3 6.1 %collective-permute-start.10 = (f32[2,7,130,1]{2,1,3,0:T(8,128)S(1)}, f32[2,7,130,1]{2,1,3,0:T(8,128)S(1)}, u32[]{:S(2)}, u32[]{:S(2)}) collective-permute-start(f32[2,7,130,1]{2,1,3,0:T(8,128)S(1)} %get-tuple-element.41), channel_id=1, source_target_pairs={{0,1},{1,2},{2,3},{3,4},{4,5},{5,6},{6,7},{8,9},{9,10},{10,11},{11... | collective-permute-start | bytes 21848 | tf_op jit(solution)/shard_map/ppermute | solution.py:27
  88.6 6.0 %copy-start.7 = (f32[7,128,128]{1,0,2:T(8,128)S(1)}, f32[7,128,128]{1,0,2:T(8,128)}, u32[]{:S(2)}) copy-start(f32[7,128,128]{1,0,2:T(8,128)} %copy.119) | copy-start | bytes 1376260
  88.7 6.0 %copy-start.10 = (f32[7,128,128]{1,0,2:T(8,128)S(1)}, f32[7,128,128]{1,0,2:T(8,128)}, u32[]{:S(2)}) copy-start(f32[7,128,128]{1,0,2:T(8,128)} %copy.124) | copy-start | bytes 1376260
  88.7 5.9 %copy-start.13 = (f32[7,128,128]{1,0,2:T(8,128)S(1)}, f32[7,128,128]{1,0,2:T(8,128)}, u32[]{:S(2)}) copy-start(f32[7,128,128]{1,0,2:T(8,128)} %copy.129) | copy-start | bytes 1376260
  88.7 5.9 %copy-start.16 = (f32[7,128,128]{1,0,2:T(8,128)S(1)}, f32[7,128,128]{1,0,2:T(8,128)}, u32[]{:S(2)}) copy-start(f32[7,128,128]{1,0,2:T(8,128)} %copy.134) | copy-start | bytes 1376260
  88.7 5.9 %copy-start.19 = (f32[7,128,128]{1,0,2:T(8,128)S(1)}, f32[7,128,128]{1,0,2:T(8,128)}, u32[]{:S(2)}) copy-start(f32[7,128,128]{1,0,2:T(8,128)} %copy.117) | copy-start | bytes 1376260
  88.7 5.9 %collective-permute-start.11 = (f32[2,7,130,1]{2,1,3,0:T(8,128)S(1)}, f32[2,7,130,1]{2,1,3,0:T(8,128)S(1)}, u32[]{:S(2)}, u32[]{:S(2)}) collective-permute-start(f32[2,7,130,1]{2,1,3,0:T(8,128)S(1)} %get-tuple-element.42), channel_id=1, source_target_pairs={{1,0},{2,1},{3,2},{4,3},{5,4},{6,5},{7,6},{9,8},{10,9},{11,10},{12... | collective-permute-start | bytes 21848 | tf_op jit(solution)/shard_map/ppermute | solution.py:28
  127.0 4.9 %collective-permute-start.12 = (f32[2,7,1,128]{3,1,2,0:T(8,128)S(1)}, f32[2,7,1,128]{3,1,2,0:T(8,128)S(1)}, u32[]{:S(2)}, u32[]{:S(2)}) collective-permute-start(f32[2,7,1,128]{3,1,2,0:T(8,128)S(1)} %copy.147), channel_id=1, source_target_pairs={{0,8},{8,16},{16,24},{1,9},{9,17},{17,25},{2,10},{10,18},{18,26},{... | collective-permute-start | bytes 21512 | tf_op jit(solution)/shard_map/ppermute | solution.py:27
  130.6 4.6 %collective-permute-start.13 = (f32[2,7,1,128]{3,1,2,0:T(8,128)S(1)}, f32[2,7,1,128]{3,1,2,0:T(8,128)S(1)}, u32[]{:S(2)}, u32[]{:S(2)}) collective-permute-start(f32[2,7,1,128]{3,1,2,0:T(8,128)S(1)} %copy.149), channel_id=1, source_target_pairs={{8,0},{16,8},{24,16},{9,1},{17,9},{25,17},{10,2},{18,10},{26,18},{... | collective-permute-start | bytes 21512 | tf_op jit(solution)/shard_map/ppermute | solution.py:28
  136.5 9.2 %copy-start.27 = (f32[2,7,1,128]{2,1,3,0:T(8,128)S(1)}, f32[2,7,1,128]{2,1,3,0:T(8,128)}, u32[]{:S(2)}) copy-start(f32[2,7,1,128]{2,1,3,0:T(8,128)} %copy.148) | copy-start | bytes 21508
  136.5 9.2 %copy-start.28 = (f32[2,7,1,128]{2,1,3,0:T(8,128)S(1)}, f32[2,7,1,128]{2,1,3,0:T(8,128)}, u32[]{:S(2)}) copy-start(f32[2,7,1,128]{2,1,3,0:T(8,128)} %copy.150) | copy-start | bytes 21508
  137.5 4.2 %collective-permute-start.14 = (f32[2,7,130,1]{2,1,3,0:T(8,128)S(1)}, f32[2,7,130,1]{2,1,3,0:T(8,128)S(1)}, u32[]{:S(2)}, u32[]{:S(2)}) collective-permute-start(f32[2,7,130,1]{2,1,3,0:T(8,128)S(1)} %get-tuple-element.39), channel_id=1, source_target_pairs={{0,1},{1,2},{2,3},{3,4},{4,5},{5,6},{6,7},{8,9},{9,10},{10,11},{11... | collective-permute-start | bytes 21848 | tf_op jit(solution)/shard_map/ppermute | solution.py:27
  139.7 6.0 %copy-start.3 = (f32[2,7,128,128]{2,1,3,0:T(8,128)S(1)}, f32[2,7,128,128]{2,1,3,0:T(8,128)}, u32[]{:S(2)}) copy-start(f32[2,7,128,128]{2,1,3,0:T(8,128)} %get-tuple-element.29) | copy-start | bytes 2752516
  139.7 6.0 %copy-start.8 = (f32[7,128,128]{1,0,2:T(8,128)S(1)}, f32[7,128,128]{1,0,2:T(8,128)}, u32[]{:S(2)}) copy-start(f32[7,128,128]{1,0,2:T(8,128)} %copy.119) | copy-start | bytes 1376260
  139.7 6.0 %copy-start.11 = (f32[7,128,128]{1,0,2:T(8,128)S(1)}, f32[7,128,128]{1,0,2:T(8,128)}, u32[]{:S(2)}) copy-start(f32[7,128,128]{1,0,2:T(8,128)} %copy.124) | copy-start | bytes 1376260
  139.7 6.0 %copy-start.14 = (f32[7,128,128]{1,0,2:T(8,128)S(1)}, f32[7,128,128]{1,0,2:T(8,128)}, u32[]{:S(2)}) copy-start(f32[7,128,128]{1,0,2:T(8,128)} %copy.129) | copy-start | bytes 1376260
  139.7 6.0 %copy-start.17 = (f32[7,128,128]{1,0,2:T(8,128)S(1)}, f32[7,128,128]{1,0,2:T(8,128)}, u32[]{:S(2)}) copy-start(f32[7,128,128]{1,0,2:T(8,128)} %copy.134) | copy-start | bytes 1376260
  139.8 6.0 %copy-start.20 = (f32[7,128,128]{1,0,2:T(8,128)S(1)}, f32[7,128,128]{1,0,2:T(8,128)}, u32[]{:S(2)}) copy-start(f32[7,128,128]{1,0,2:T(8,128)} %copy.117) | copy-start | bytes 1376260
  139.8 5.9 %collective-permute-start.15 = (f32[2,7,130,1]{2,1,3,0:T(8,128)S(1)}, f32[2,7,130,1]{2,1,3,0:T(8,128)S(1)}, u32[]{:S(2)}, u32[]{:S(2)}) collective-permute-start(f32[2,7,130,1]{2,1,3,0:T(8,128)S(1)} %get-tuple-element.40), channel_id=1, source_target_pairs={{1,0},{2,1},{3,2},{4,3},{5,4},{6,5},{7,6},{9,8},{10,9},{11,10},{12... | collective-permute-start | bytes 21848 | tf_op jit(solution)/shard_map/ppermute | solution.py:28
  181.0 7.9 %collective-permute-start.17 = (f32[2,7,1,128]{3,1,2,0:T(8,128)S(1)}, f32[2,7,1,128]{3,1,2,0:T(8,128)S(1)}, u32[]{:S(2)}, u32[]{:S(2)}) collective-permute-start(f32[2,7,1,128]{3,1,2,0:T(8,128)S(1)} %copy.155), channel_id=1, source_target_pairs={{8,0},{16,8},{24,16},{9,1},{17,9},{25,17},{10,2},{18,10},{26,18},{... | collective-permute-start | bytes 21512 | tf_op jit(solution)/shard_map/ppermute | solution.py:28
  182.3 5.2 %collective-permute-start.16 = (f32[2,7,1,128]{3,1,2,0:T(8,128)S(1)}, f32[2,7,1,128]{3,1,2,0:T(8,128)S(1)}, u32[]{:S(2)}, u32[]{:S(2)}) collective-permute-start(f32[2,7,1,128]{3,1,2,0:T(8,128)S(1)} %copy.153), channel_id=1, source_target_pairs={{0,8},{8,16},{16,24},{1,9},{9,17},{17,25},{2,10},{10,18},{18,26},{... | collective-permute-start | bytes 21512 | tf_op jit(solution)/shard_map/ppermute | solution.py:27
  190.3 9.6 %copy-start.18 = (f32[7,128,128]{1,0,2:T(8,128)S(1)}, f32[7,128,128]{1,0,2:T(8,128)}, u32[]{:S(2)}) copy-start(f32[7,128,128]{1,0,2:T(8,128)} %copy.134) | copy-start | bytes 1376260
  190.3 9.6 %copy-start.21 = (f32[7,128,128]{1,0,2:T(8,128)S(1)}, f32[7,128,128]{1,0,2:T(8,128)}, u32[]{:S(2)}) copy-start(f32[7,128,128]{1,0,2:T(8,128)} %copy.117) | copy-start | bytes 1376260
  191.3 4.6 %collective-permute-start.18 = (f32[2,7,130,1]{2,1,3,0:T(8,128)S(1)}, f32[2,7,130,1]{2,1,3,0:T(8,128)S(1)}, u32[]{:S(2)}, u32[]{:S(2)}) collective-permute-start(f32[2,7,130,1]{2,1,3,0:T(8,128)S(1)} %get-tuple-element.37), channel_id=1, source_target_pairs={{0,1},{1,2},{2,3},{3,4},{4,5},{5,6},{6,7},{8,9},{9,10},{10,11},{11... | collective-permute-start | bytes 21848 | tf_op jit(solution)/shard_map/ppermute | solution.py:27
  194.3 5.6 %collective-permute-start.19 = (f32[2,7,130,1]{2,1,3,0:T(8,128)S(1)}, f32[2,7,130,1]{2,1,3,0:T(8,128)S(1)}, u32[]{:S(2)}, u32[]{:S(2)}) collective-permute-start(f32[2,7,130,1]{2,1,3,0:T(8,128)S(1)} %get-tuple-element.38), channel_id=1, source_target_pairs={{1,0},{2,1},{3,2},{4,3},{5,4},{6,5},{7,6},{9,8},{10,9},{11,10},{12... | collective-permute-start | bytes 21848 | tf_op jit(solution)/shard_map/ppermute | solution.py:28
  (17 other events, 50.2 us)
